TPU v7x, 32 devices: a whole 2x2x4 slice. The times are simulated.
32 devices in a mesh: tm: 4 (over y, x), space: 8 (over z, core).
Axes of the slice: x: 2, y: 2, z: 4, core: 2. Of those that a mesh axis runs over, the one named last changes fastest.
Arguments:
- initial_state: float32 [3, 192, 256], P(None, 'space'), may hold values from -2 to 2
- c_guess: float32 [4, 3, 192, 256], P('tm', None, 'space'), may hold values from -2 to 2
- friction: float32 [192, 256], P('space'), may hold values from 0.05 to 1
Outputs:
- c_points: float32 [4, 3, 192, 256], P('tm', None, 'space')
- f_points: float32 [4, 3, 192, 256], P('tm', None, 'space')
All inputs are finite; a program needn't handle non-finite values.
Results may differ from a plain program's by a relative error of at most 0.00012.
Values sent between devices are 32-bit elements; how exact they have to be, the bound alone decides.
No kernel may reach another device: no remote copies, remote signals or barrier semaphores. Data moves between devices by JAX's collectives and lax.ppermute only.
A program may use at most 64 MiB of HBM per device.

v0:
```python
import jax
import jax.numpy as jnp
from jax import lax
from jax.sharding import PartitionSpec as P

STEPS = 8
gravity = 2.0
coriolis = 0.5
viscosity = 0.5
time_step = 0.04


def with_halo(block, sides, width):
    for axis, dim in sides:
        count = lax.axis_size(axis)
        forward = [(i, i + 1) for i in range(count - 1)]
        forward.append((count - 1, 0))
        backward = [(target, source) for source, target in forward]
        low = lax.ppermute(
            lax.slice_in_dim(block, block.shape[dim] - width, None, axis=dim), axis, forward
        )
        high = lax.ppermute(lax.slice_in_dim(block, 0, width, axis=dim), axis, backward)
        block = jnp.concatenate([low, block, high], axis=dim)
    return block


def shifted(value, axis, by):
    size = lax.axis_size(axis)
    pairs = [(i, i + by) for i in range(size) if 0 <= i + by < size]
    return lax.ppermute(value, axis, pairs)


def cut_neighbours(field):
    return (
        field[2:],
        field[:-2],
        jnp.roll(field, -1, 1)[1:-1],
        jnp.roll(field, 1, 1)[1:-1],
        field[1:-1],
    )


def spread(near):
    return near[0] + near[1] + near[2] + near[3] - 4.0 * near[4]


def tendency(fields, drag, neighbours):
    height = fields[0]
    row_vel = fields[1]
    col_vel = fields[2]
    height_near = neighbours(height)
    row_near = neighbours(row_vel)
    col_near = neighbours(col_vel)
    flux_row = neighbours((1.0 + height) * row_vel)
    flux_col = neighbours((1.0 + height) * col_vel)
    row_mid = row_near[4]
    col_mid = col_near[4]
    rate_height = -(
        0.5 * (flux_row[0] - flux_row[1]) + 0.5 * (flux_col[2] - flux_col[3])
    ) + viscosity * spread(height_near)
    rate_row = (
        -(
            row_mid * (0.5 * (row_near[0] - row_near[1]))
            + col_mid * (0.5 * (row_near[2] - row_near[3]))
        )
        - gravity * (0.5 * (height_near[0] - height_near[1]))
        + coriolis * col_mid
        - drag * row_mid
        + viscosity * spread(row_near)
    )
    rate_col = (
        -(
            row_mid * (0.5 * (col_near[0] - col_near[1]))
            + col_mid * (0.5 * (col_near[2] - col_near[3]))
        )
        - gravity * (0.5 * (height_near[2] - height_near[3]))
        - coriolis * row_mid
        - drag * col_mid
        + viscosity * spread(col_near)
    )
    return jnp.stack([rate_height, rate_row, rate_col])


def trim_rows(array, width):
    return array[..., width : array.shape[-2] - width, :]


def heun_step(fields, drag, size):
    slope_one = tendency(fields, drag[1:-1], cut_neighbours)
    midpoint = fields[:, 1:-1] + size * slope_one
    slope_two = tendency(midpoint, drag[2:-2], cut_neighbours)
    return fields[:, 2:-2] + 0.5 * size * (slope_one[:, 1:-1] + slope_two)


def advance(fields, drag_pad, step_count, layers, with_coarse):
    coarse = fields
    reaches = [layers] * (step_count // layers)
    if step_count % layers:
        reaches = reaches + [step_count % layers]
    for group, reach in enumerate(reaches):
        padded = with_halo(fields, (("space", 1),), 2 * reach)
        drag = trim_rows(drag_pad, 8 - 2 * reach)
        if with_coarse and group == 0:
            coarse = trim_rows(heun_step(padded, drag, STEPS * time_step), 2 * reach - 2)
        for repeat in range(reach):
            padded = heun_step(padded, drag, time_step)
            drag = trim_rows(drag, 2)
        fields = padded
    return (fields, coarse)


def body(initial_state, c_guess, friction):
    slice_index = lax.axis_index("tm")
    coarse_step = STEPS * time_step
    layers = 4
    drag_pad = with_halo(friction, (("space", 0),), 8)

    def earlier(fields):
        incoming = shifted(fields, "tm", 1)
        return jnp.where(slice_index == 0, initial_state, incoming)

    relaxed, unused = advance(earlier(c_guess[0]), drag_pad, STEPS, layers, False)
    fine_end, coarse_end = advance(earlier(relaxed), drag_pad, STEPS, layers, True)
    defect = fine_end - coarse_end
    defect_pad = with_halo(defect, (("space", 1),), 8)
    gathered = lax.all_gather(defect_pad[None], "tm", axis=0, tiled=True)

    def group_fn(group, carry):
        current, owned = carry
        padded = with_halo(current, (("space", 1),), 8)
        drag = drag_pad
        for offset in range(4):
            turn = group * 4 + offset
            defect_now = trim_rows(
                lax.dynamic_index_in_dim(gathered, turn, 0, keepdims=False), 2 * offset + 2
            )
            padded = heun_step(padded, drag, coarse_step) + defect_now
            drag = trim_rows(drag, 2)
            owned = jnp.where(turn == slice_index, trim_rows(padded, 6 - 2 * offset), owned)
        return (padded, owned)

    unused_state, c_points = lax.fori_loop(
        0, lax.axis_size("tm") // 4, group_fn, (initial_state, jnp.zeros_like(defect))
    )
    f_points, unused_end = advance(earlier(c_points), drag_pad, STEPS - 1, layers, False)
    return (c_points[None], f_points[None])


def solution(mesh):
    placed = (P(None, "space", None), P("tm", None, "space", None), P("space", None))
    return jax.shard_map(
        body,
        mesh=mesh,
        in_specs=placed,
        out_specs=(P("tm", None, "space", None), P("tm", None, "space", None)),
        check_vma=False,
    )
```

profile of v0, /device:TPU:4, one launch (start us, length us, event | category | flops | bytes accessed | tf_op | source)
XLA Modules:
  0.0 128.7 jit_solution(17374172756652679504)
XLA Ops:
  1.4 0.8 fusion.1657
  2.2 1.7 %collective-permute-start = (f32[3,8,256]{2,1,0:T(8,128)S(1)}, f32[3,8,256]{2,1,0:T(8,128)S(1)}, u32[]{:S(2)}, u32[]{:S(2)}) collective-permute-start(f32[3,8,256]{2,1,0:T(8,128)S(1)} %get-tuple-element.361), channel_id=1, source_target_pairs={{0,1},{1,2},{2,3},{3,4},{4,5},{5,6},{6,7},{7,0},{8,9},{9,10},{10,1... | collective-permute-start | bytes 73736 | tf_op jit(solution)/shard_map/while/body/eval_jaxpr/ppermute | solution.py:19
  3.8 3.4 %collective-permute-start.4 = (f32[3,24,256]{2,1,0:T(8,128)S(1)}, f32[3,24,256]{2,1,0:T(8,128)S(1)}, u32[]{:S(2)}, u32[]{:S(2)}) collective-permute-start(f32[3,24,256]{2,1,0:T(8,128)S(1)} %bitcast.5615), channel_id=1, source_target_pairs={{0,8},{8,16},{16,24},{1,9},{9,17},{17,25},{2,10},{10,18},{18,26},{... | collective-permute-start | bytes 221192 | tf_op jit(solution)/shard_map/ppermute | solution.py:30
  7.2 1.6 %collective-permute-start.3 = (f32[8,256]{1,0:T(8,128)S(1)}, f32[8,256]{1,0:T(8,128)S(1)}, u32[]{:S(2)}, u32[]{:S(2)}) collective-permute-start(f32[8,256]{1,0:T(8,128)S(1)} %get-tuple-element.1254), channel_id=1, source_target_pairs={{1,0},{2,1},{3,2},{4,3},{5,4},{6,5},{7,6},{0,7},{9,8},{10,9},{11,1... | collective-permute-start | bytes 24584 | tf_op jit(solution)/shard_map/ppermute | solution.py:22
  8.9 0.8 collective-permute-start.1
  12.3 3.6 %collective-permute-start.6 = (f32[3,8,256]{2,1,0:T(8,128)S(1)}, f32[3,8,256]{2,1,0:T(8,128)S(1)}, u32[]{:S(2)}, u32[]{:S(2)}) collective-permute-start(f32[3,8,256]{2,1,0:T(8,128)S(1)} %get-tuple-element.373), channel_id=1, source_target_pairs={{1,0},{2,1},{3,2},{4,3},{5,4},{6,5},{7,6},{0,7},{9,8},{10,9},{11,1... | collective-permute-start | bytes 73736 | tf_op jit(solution)/shard_map/ppermute | solution.py:22
  16.3 1.1 collective-permute-done.6
  17.4 3.5 %collective-permute-done.5 = f32[3,8,256]{2,1,0:T(8,128)S(1)} collective-permute-done((f32[3,8,256]{2,1,0:T(8,128)S(1)}, f32[3,8,256]{2,1,0:T(8,128)S(1)}, u32[]{:S(2)}, u32[]{:S(2)}) %collective-permute-start.5) | collective-permute-done | bytes 24608 | tf_op jit(solution)/shard_map/ppermute | solution.py:19
  29.4 0.9 collective-permute-done.8
  30.4 3.6 %collective-permute-done.7 = f32[3,8,256]{2,1,0:T(8,128)S(1)} collective-permute-done((f32[3,8,256]{2,1,0:T(8,128)S(1)}, f32[3,8,256]{2,1,0:T(8,128)S(1)}, u32[]{:S(2)}, u32[]{:S(2)}) %collective-permute-start.7) | collective-permute-done | bytes 24608 | tf_op jit(solution)/shard_map/ppermute | solution.py:19
  42.0 1.9 %collective-permute-start.9 = (f32[3,24,256]{2,1,0:T(8,128)S(1)}, f32[3,24,256]{2,1,0:T(8,128)S(1)}, u32[]{:S(2)}, u32[]{:S(2)}) collective-permute-start(f32[3,24,256]{2,1,0:T(8,128)S(1)} %fusion.57), channel_id=1, source_target_pairs={{0,8},{8,16},{16,24},{1,9},{9,17},{17,25},{2,10},{10,18},{18,26},{... | collective-permute-start | bytes 221192 | tf_op jit(solution)/shard_map/ppermute | solution.py:30
  44.1 5.1 %collective-permute-done.9 = f32[3,24,256]{2,1,0:T(8,128)S(1)} collective-permute-done((f32[3,24,256]{2,1,0:T(8,128)S(1)}, f32[3,24,256]{2,1,0:T(8,128)S(1)}, u32[]{:S(2)}, u32[]{:S(2)}) %collective-permute-start.9) | collective-permute-done | bytes 73760 | tf_op jit(solution)/shard_map/ppermute | solution.py:30
  49.8 0.9 collective-permute-done.11
  50.8 3.6 %collective-permute-done.10 = f32[3,8,256]{2,1,0:T(8,128)S(1)} collective-permute-done((f32[3,8,256]{2,1,0:T(8,128)S(1)}, f32[3,8,256]{2,1,0:T(8,128)S(1)}, u32[]{:S(2)}, u32[]{:S(2)}) %collective-permute-start.10) | collective-permute-done | bytes 24608 | tf_op jit(solution)/shard_map/ppermute | solution.py:19
  64.7 3.7 %collective-permute-done.12 = f32[3,8,256]{2,1,0:T(8,128)S(1)} collective-permute-done((f32[3,8,256]{2,1,0:T(8,128)S(1)}, f32[3,8,256]{2,1,0:T(8,128)S(1)}, u32[]{:S(2)}, u32[]{:S(2)}) %collective-permute-start.12) | collective-permute-done | bytes 24608 | tf_op jit(solution)/shard_map/ppermute | solution.py:19
  77.2 0.9 collective-permute-done.15
  78.1 3.6 %collective-permute-done.14 = f32[3,8,256]{2,1,0:T(8,128)S(1)} collective-permute-done((f32[3,8,256]{2,1,0:T(8,128)S(1)}, f32[3,8,256]{2,1,0:T(8,128)S(1)}, u32[]{:S(2)}, u32[]{:S(2)}) %collective-permute-start.14) | collective-permute-done | bytes 24608 | tf_op jit(solution)/shard_map/ppermute | solution.py:19
  81.7 8.7 %all-gather = f32[12,40,256]{2,1,0:T(8,128)S(1)} all-gather(f32[3,40,256]{2,1,0:T(8,128)S(1)} %pad_maximum_fusion.13), channel_id=2, replica_groups=mesh['tm'=4,'space'=8] {'tm'}, dimensions={0}, use_global_device_ids=true | all-gather | bytes 614400 | tf_op jit(solution)/shard_map/all_gather | solution.py:126
  96.5 3.6 %collective-permute-start.16 = (f32[3,24,256]{2,1,0:T(8,128)S(1)}, f32[3,24,256]{2,1,0:T(8,128)S(1)}, u32[]{:S(2)}, u32[]{:S(2)}) collective-permute-start(f32[3,24,256]{2,1,0:T(8,128)S(1)} %fusion.47), channel_id=1, source_target_pairs={{0,8},{8,16},{16,24},{1,9},{9,17},{17,25},{2,10},{10,18},{18,26},{... | collective-permute-start | bytes 221192 | tf_op jit(solution)/shard_map/ppermute | solution.py:30
  100.1 3.5 %collective-permute-done.16 = f32[3,24,256]{2,1,0:T(8,128)S(1)} collective-permute-done((f32[3,24,256]{2,1,0:T(8,128)S(1)}, f32[3,24,256]{2,1,0:T(8,128)S(1)}, u32[]{:S(2)}, u32[]{:S(2)}) %collective-permute-start.16) | collective-permute-done | bytes 73760 | tf_op jit(solution)/shard_map/ppermute | solution.py:30
  104.2 1.0 collective-permute-done.18
  105.3 3.6 %collective-permute-done.17 = f32[3,8,256]{2,1,0:T(8,128)S(1)} collective-permute-done((f32[3,8,256]{2,1,0:T(8,128)S(1)}, f32[3,8,256]{2,1,0:T(8,128)S(1)}, u32[]{:S(2)}, u32[]{:S(2)}) %collective-permute-start.17) | collective-permute-done | bytes 24608 | tf_op jit(solution)/shard_map/ppermute | solution.py:19
  117.5 1.0 collective-permute-done.20
  118.5 3.6 %collective-permute-done.19 = f32[3,6,256]{2,1,0:T(8,128)S(1)} collective-permute-done((f32[3,6,256]{2,1,0:T(8,128)S(1)}, f32[3,6,256]{2,1,0:T(8,128)S(1)}, u32[]{:S(2)}, u32[]{:S(2)}) %collective-permute-start.19) | collective-permute-done | bytes 18464 | tf_op jit(solution)/shard_map/ppermute | solution.py:19
  (816 shorter events, 60.1 us)
Async XLA Ops:
  0.6 3.2 %copy-start.3 = (f32[1,3,24,256]{3,2,1,0:T(8,128)S(1)}, f32[1,3,24,256]{3,2,1,0:T(8,128)}, u32[]{:S(2)}) copy-start(f32[1,3,24,256]{3,2,1,0:T(8,128)} %param.4) | copy-start | bytes 221188
  1.4 8.3 %collective-permute-start.2 = (f32[8,256]{1,0:T(8,128)S(1)}, f32[8,256]{1,0:T(8,128)S(1)}, u32[]{:S(2)}, u32[]{:S(2)}) collective-permute-start(f32[8,256]{1,0:T(8,128)S(1)} %get-tuple-element.1255), channel_id=1, source_target_pairs={{0,1},{1,2},{2,3},{3,4},{4,5},{5,6},{6,7},{7,0},{8,9},{9,10},{10,1... | collective-permute-start | bytes 24584 | tf_op jit(solution)/shard_map/ppermute | solution.py:19
  2.2 7.5 %copy-start = (f32[24,256]{1,0:T(8,128)S(1)}, f32[24,256]{1,0:T(8,128)}, u32[]{:S(2)}) copy-start(f32[24,256]{1,0:T(8,128)} %param.5) | copy-start | bytes 73732
  2.2 8.1 %collective-permute-start = (f32[3,8,256]{2,1,0:T(8,128)S(1)}, f32[3,8,256]{2,1,0:T(8,128)S(1)}, u32[]{:S(2)}, u32[]{:S(2)}) collective-permute-start(f32[3,8,256]{2,1,0:T(8,128)S(1)} %get-tuple-element.361), channel_id=1, source_target_pairs={{0,1},{1,2},{2,3},{3,4},{4,5},{5,6},{6,7},{7,0},{8,9},{9,10},{10,1... | collective-permute-start | bytes 73736 | tf_op jit(solution)/shard_map/while/body/eval_jaxpr/ppermute | solution.py:19
  3.8 7.1 %collective-permute-start.4 = (f32[3,24,256]{2,1,0:T(8,128)S(1)}, f32[3,24,256]{2,1,0:T(8,128)S(1)}, u32[]{:S(2)}, u32[]{:S(2)}) collective-permute-start(f32[3,24,256]{2,1,0:T(8,128)S(1)} %bitcast.5615), channel_id=1, source_target_pairs={{0,8},{8,16},{16,24},{1,9},{9,17},{17,25},{2,10},{10,18},{18,26},{... | collective-permute-start | bytes 221192 | tf_op jit(solution)/shard_map/ppermute | solution.py:30
  7.2 3.0 %collective-permute-start.3 = (f32[8,256]{1,0:T(8,128)S(1)}, f32[8,256]{1,0:T(8,128)S(1)}, u32[]{:S(2)}, u32[]{:S(2)}) collective-permute-start(f32[8,256]{1,0:T(8,128)S(1)} %get-tuple-element.1254), channel_id=1, source_target_pairs={{1,0},{2,1},{3,2},{4,3},{5,4},{6,5},{7,6},{0,7},{9,8},{10,9},{11,1... | collective-permute-start | bytes 24584 | tf_op jit(solution)/shard_map/ppermute | solution.py:22
  8.9 2.3 %collective-permute-start.1 = (f32[3,8,256]{2,1,0:T(8,128)S(1)}, f32[3,8,256]{2,1,0:T(8,128)S(1)}, u32[]{:S(2)}, u32[]{:S(2)}) collective-permute-start(f32[3,8,256]{2,1,0:T(8,128)S(1)} %get-tuple-element.360), channel_id=1, source_target_pairs={{1,0},{2,1},{3,2},{4,3},{5,4},{6,5},{7,6},{0,7},{9,8},{10,9},{11,1... | collective-permute-start | bytes 73736 | tf_op jit(solution)/shard_map/while/body/eval_jaxpr/ppermute | solution.py:22
  12.3 5.1 %collective-permute-start.6 = (f32[3,8,256]{2,1,0:T(8,128)S(1)}, f32[3,8,256]{2,1,0:T(8,128)S(1)}, u32[]{:S(2)}, u32[]{:S(2)}) collective-permute-start(f32[3,8,256]{2,1,0:T(8,128)S(1)} %get-tuple-element.373), channel_id=1, source_target_pairs={{1,0},{2,1},{3,2},{4,3},{5,4},{6,5},{7,6},{0,7},{9,8},{10,9},{11,1... | collective-permute-start | bytes 73736 | tf_op jit(solution)/shard_map/ppermute | solution.py:22
  15.8 5.0 %collective-permute-start.5 = (f32[3,8,256]{2,1,0:T(8,128)S(1)}, f32[3,8,256]{2,1,0:T(8,128)S(1)}, u32[]{:S(2)}, u32[]{:S(2)}) collective-permute-start(f32[3,8,256]{2,1,0:T(8,128)S(1)} %get-tuple-element.372), channel_id=1, source_target_pairs={{0,1},{1,2},{2,3},{3,4},{4,5},{5,6},{6,7},{7,0},{8,9},{9,10},{10,1... | collective-permute-start | bytes 73736 | tf_op jit(solution)/shard_map/ppermute | solution.py:19
  28.8 1.6 %collective-permute-start.8 = (f32[3,8,256]{2,1,0:T(8,128)S(1)}, f32[3,8,256]{2,1,0:T(8,128)S(1)}, u32[]{:S(2)}, u32[]{:S(2)}) collective-permute-start(f32[3,8,256]{2,1,0:T(8,128)S(1)} %get-tuple-element.371), channel_id=1, source_target_pairs={{1,0},{2,1},{3,2},{4,3},{5,4},{6,5},{7,6},{0,7},{9,8},{10,9},{11,1... | collective-permute-start | bytes 73736 | tf_op jit(solution)/shard_map/ppermute | solution.py:22
  28.9 5.1 %collective-permute-start.7 = (f32[3,8,256]{2,1,0:T(8,128)S(1)}, f32[3,8,256]{2,1,0:T(8,128)S(1)}, u32[]{:S(2)}, u32[]{:S(2)}) collective-permute-start(f32[3,8,256]{2,1,0:T(8,128)S(1)} %get-tuple-element.370), channel_id=1, source_target_pairs={{0,1},{1,2},{2,3},{3,4},{4,5},{5,6},{6,7},{7,0},{8,9},{9,10},{10,1... | collective-permute-start | bytes 73736 | tf_op jit(solution)/shard_map/ppermute | solution.py:19
  42.0 7.1 %collective-permute-start.9 = (f32[3,24,256]{2,1,0:T(8,128)S(1)}, f32[3,24,256]{2,1,0:T(8,128)S(1)}, u32[]{:S(2)}, u32[]{:S(2)}) collective-permute-start(f32[3,24,256]{2,1,0:T(8,128)S(1)} %fusion.57), channel_id=1, source_target_pairs={{0,8},{8,16},{16,24},{1,9},{9,17},{17,25},{2,10},{10,18},{18,26},{... | collective-permute-start | bytes 221192 | tf_op jit(solution)/shard_map/ppermute | solution.py:30
  49.2 1.6 %collective-permute-start.11 = (f32[3,8,256]{2,1,0:T(8,128)S(1)}, f32[3,8,256]{2,1,0:T(8,128)S(1)}, u32[]{:S(2)}, u32[]{:S(2)}) collective-permute-start(f32[3,8,256]{2,1,0:T(8,128)S(1)} %get-tuple-element.369), channel_id=1, source_target_pairs={{1,0},{2,1},{3,2},{4,3},{5,4},{6,5},{7,6},{0,7},{9,8},{10,9},{11,1... | collective-permute-start | bytes 73736 | tf_op jit(solution)/shard_map/ppermute | solution.py:22
  49.3 5.1 %collective-permute-start.10 = (f32[3,8,256]{2,1,0:T(8,128)S(1)}, f32[3,8,256]{2,1,0:T(8,128)S(1)}, u32[]{:S(2)}, u32[]{:S(2)}) collective-permute-start(f32[3,8,256]{2,1,0:T(8,128)S(1)} %get-tuple-element.368), channel_id=1, source_target_pairs={{0,1},{1,2},{2,3},{3,4},{4,5},{5,6},{6,7},{7,0},{8,9},{9,10},{10,1... | collective-permute-start | bytes 73736 | tf_op jit(solution)/shard_map/ppermute | solution.py:19
  63.1 1.6 %collective-permute-start.13 = (f32[3,8,256]{2,1,0:T(8,128)S(1)}, f32[3,8,256]{2,1,0:T(8,128)S(1)}, u32[]{:S(2)}, u32[]{:S(2)}) collective-permute-start(f32[3,8,256]{2,1,0:T(8,128)S(1)} %get-tuple-element.367), channel_id=1, source_target_pairs={{1,0},{2,1},{3,2},{4,3},{5,4},{6,5},{7,6},{0,7},{9,8},{10,9},{11,1... | collective-permute-start | bytes 73736 | tf_op jit(solution)/shard_map/ppermute | solution.py:22
  63.2 5.3 %collective-permute-start.12 = (f32[3,8,256]{2,1,0:T(8,128)S(1)}, f32[3,8,256]{2,1,0:T(8,128)S(1)}, u32[]{:S(2)}, u32[]{:S(2)}) collective-permute-start(f32[3,8,256]{2,1,0:T(8,128)S(1)} %get-tuple-element.366), channel_id=1, source_target_pairs={{0,1},{1,2},{2,3},{3,4},{4,5},{5,6},{6,7},{7,0},{8,9},{9,10},{10,1... | collective-permute-start | bytes 73736 | tf_op jit(solution)/shard_map/ppermute | solution.py:19
  76.5 1.6 %collective-permute-start.15 = (f32[3,8,256]{2,1,0:T(8,128)S(1)}, f32[3,8,256]{2,1,0:T(8,128)S(1)}, u32[]{:S(2)}, u32[]{:S(2)}) collective-permute-start(f32[3,8,256]{2,1,0:T(8,128)S(1)} %get-tuple-element.365), channel_id=1, source_target_pairs={{1,0},{2,1},{3,2},{4,3},{5,4},{6,5},{7,6},{0,7},{9,8},{10,9},{11,1... | collective-permute-start | bytes 73736 | tf_op jit(solution)/shard_map/ppermute | solution.py:22
  76.6 5.1 %collective-permute-start.14 = (f32[3,8,256]{2,1,0:T(8,128)S(1)}, f32[3,8,256]{2,1,0:T(8,128)S(1)}, u32[]{:S(2)}, u32[]{:S(2)}) collective-permute-start(f32[3,8,256]{2,1,0:T(8,128)S(1)} %get-tuple-element.364), channel_id=1, source_target_pairs={{0,1},{1,2},{2,3},{3,4},{4,5},{5,6},{6,7},{7,0},{8,9},{9,10},{10,1... | collective-permute-start | bytes 73736 | tf_op jit(solution)/shard_map/ppermute | solution.py:19
  96.5 7.2 %copy-start.2 = (f32[3,24,256]{2,1,0:T(8,128)}, f32[3,24,256]{2,1,0:T(8,128)S(1)}, u32[]{:S(2)}) copy-start(f32[3,24,256]{2,1,0:T(8,128)S(1)} %fusion.47) | copy-start | bytes 221188
  96.5 7.1 %collective-permute-start.16 = (f32[3,24,256]{2,1,0:T(8,128)S(1)}, f32[3,24,256]{2,1,0:T(8,128)S(1)}, u32[]{:S(2)}, u32[]{:S(2)}) collective-permute-start(f32[3,24,256]{2,1,0:T(8,128)S(1)} %fusion.47), channel_id=1, source_target_pairs={{0,8},{8,16},{16,24},{1,9},{9,17},{17,25},{2,10},{10,18},{18,26},{... | collective-permute-start | bytes 221192 | tf_op jit(solution)/shard_map/ppermute | solution.py:30
  103.7 1.6 %collective-permute-start.18 = (f32[3,8,256]{2,1,0:T(8,128)S(1)}, f32[3,8,256]{2,1,0:T(8,128)S(1)}, u32[]{:S(2)}, u32[]{:S(2)}) collective-permute-start(f32[3,8,256]{2,1,0:T(8,128)S(1)} %get-tuple-element.359), channel_id=1, source_target_pairs={{1,0},{2,1},{3,2},{4,3},{5,4},{6,5},{7,6},{0,7},{9,8},{10,9},{11,1... | collective-permute-start | bytes 73736 | tf_op jit(solution)/shard_map/ppermute | solution.py:22
  103.7 5.1 %collective-permute-start.17 = (f32[3,8,256]{2,1,0:T(8,128)S(1)}, f32[3,8,256]{2,1,0:T(8,128)S(1)}, u32[]{:S(2)}, u32[]{:S(2)}) collective-permute-start(f32[3,8,256]{2,1,0:T(8,128)S(1)} %get-tuple-element.358), channel_id=1, source_target_pairs={{0,1},{1,2},{2,3},{3,4},{4,5},{5,6},{6,7},{7,0},{8,9},{9,10},{10,1... | collective-permute-start | bytes 73736 | tf_op jit(solution)/shard_map/ppermute | solution.py:19
  116.9 1.6 %collective-permute-start.20 = (f32[3,6,256]{2,1,0:T(8,128)S(1)}, f32[3,6,256]{2,1,0:T(8,128)S(1)}, u32[]{:S(2)}, u32[]{:S(2)}) collective-permute-start(f32[3,6,256]{2,1,0:T(8,128)S(1)} %get-tuple-element.357), channel_id=1, source_target_pairs={{1,0},{2,1},{3,2},{4,3},{5,4},{6,5},{7,6},{0,7},{9,8},{10,9},{11,1... | collective-permute-start | bytes 55304 | tf_op jit(solution)/shard_map/ppermute | solution.py:22
  117.0 5.1 %collective-permute-start.19 = (f32[3,6,256]{2,1,0:T(8,128)S(1)}, f32[3,6,256]{2,1,0:T(8,128)S(1)}, u32[]{:S(2)}, u32[]{:S(2)}) collective-permute-start(f32[3,6,256]{2,1,0:T(8,128)S(1)} %get-tuple-element.356), channel_id=1, source_target_pairs={{0,1},{1,2},{2,3},{3,4},{4,5},{5,6},{6,7},{7,0},{8,9},{9,10},{10,1... | collective-permute-start | bytes 55304 | tf_op jit(solution)/shard_map/ppermute | solution.py:19
  (1 other events, 1.3 us)
where the time goes:
time: 129 us
  waiting for transfers between devices  41.9 us (32%)
  local copies, waits for them, and re-layouts  34.5 us (27%)
  other arithmetic  20.8 us (16%)
  starting transfers between devices  20 us (16%)
  blocking collectives  8.68 us (7%)
  between operations  2.78 us (2%)
    ppermute x9, waiting for transfers between devices, with_halo(): lax.ppermute(lax.slice_in_dim(block, block.shape[dim] - width, None, axis...  25.2 us
    slice x326, local copies, waits for them, and re-layouts, cut_neighbours(): jnp.roll(field, 1, 1)[1:-1]  24.3 us
    another operation x165, other arithmetic, tendency(): return jnp.stack([rate_height, rate_row, rate_col])  17.3 us
    ppermute x3, waiting for transfers between devices, shifted(): return lax.ppermute(value, axis, pairs)  9.3 us
    ppermute x3, starting transfers between devices, shifted(): return lax.ppermute(value, axis, pairs)  8.96 us
    all_gather x1, blocking collectives, body(): gathered = lax.all_gather(defect_pad[None], 'tm', axis=0, tiled=True)  8.68 us
    slice x110, local copies, waits for them, and re-layouts, cut_neighbours(): jnp.roll(field, -1, 1)[1:-1]  8.11 us
    ppermute x9, waiting for transfers between devices, with_halo(): lax.ppermute(lax.slice_in_dim(block, 0, width, axis=dim), axis, backward)  7.4 us
  transfers between devices with their start and end apart: 21, of which 19 were waited for; matrix products, arithmetic and copies ran while one was open for 1% of the time, Pallas kernels for 0%

commit v1 on v0

--- a/solution.py
+++ b/solution.py
@@ -123,7 +123,20 @@
     fine_end, coarse_end = advance(earlier(relaxed), drag_pad, STEPS, layers, True)
     defect = fine_end - coarse_end
     defect_pad = with_halo(defect, (("space", 1),), 8)
-    gathered = lax.all_gather(defect_pad[None], "tm", axis=0, tiled=True)
+    here_x = defect_pad[None]
+    chips = lax.axis_size("tm")
+    y2 = sorted(((s, (s + 1) % chips) for s in range(chips)))
+    far_arr = here_x
+    grid = [far_arr]
+    ix = 1
+    while ix < chips:
+        far_arr = lax.ppermute(far_arr, "tm", y2)
+        grid.insert(0, far_arr)
+        ix += 1
+    mixed_arr = jnp.concatenate(grid, axis=0)
+    state_next = lax.axis_index("tm")
+    built = state_next + 1
+    gathered = jnp.roll(mixed_arr, shift=built * here_x.shape[0], axis=0)
 
     def group_fn(group, carry):
         current, owned = carry

time: 129 us -> 139 us (1.078)
  waiting for transfers between devices: 41.9 us -> 61.6 us
  blocking collectives: 8.68 us -> 0 us
  starting transfers between devices: 20 us -> 18.3 us
    ppermute x0 -> x3, waiting for transfers between devices: none -> 18.5 us  [body(): far_arr = lax.ppermute(far_arr, 'tm', y2)]
    all_gather x1 -> x0, blocking collectives: 8.68 us -> none  [body(): gathered = lax.all_gather(defect_pad[None], 'tm', axis=0, tiled=True)]
    ppermute x3, starting transfers between devices: 8.96 us -> 7.23 us  [shifted(): return lax.ppermute(value, axis, pairs)]
    ppermute x3, waiting for transfers between devices: 9.3 us -> 10.9 us  [shifted(): return lax.ppermute(value, axis, pairs)]
  transfers between devices with their start and end apart: 21 -> 24, of which waited for: 19 -> 21; matrix products, arithmetic and copies ran while one was open for 1% -> 1% of each run, Pallas kernels for 0% -> 0%
where the time goes in v1:
time: 139 us
  waiting for transfers between devices  61.6 us (44%)
  local copies, waits for them, and re-layouts  35.4 us (25%)
  other arithmetic  20.8 us (15%)
  starting transfers between devices  18.3 us (13%)
  between operations  2.84 us (2%)
    ppermute x9, waiting for transfers between devices, with_halo(): lax.ppermute(lax.slice_in_dim(block, block.shape[dim] - width, None, axis...  25.2 us
    slice x326, local copies, waits for them, and re-layouts, cut_neighbours(): jnp.roll(field, 1, 1)[1:-1]  24.3 us
    ppermute x3, waiting for transfers between devices, body(): far_arr = lax.ppermute(far_arr, 'tm', y2)  18.5 us
    another operation x165, other arithmetic, tendency(): return jnp.stack([rate_height, rate_row, rate_col])  17.3 us
    ppermute x3, waiting for transfers between devices, shifted(): return lax.ppermute(value, axis, pairs)  10.9 us
    slice x110, local copies, waits for them, and re-layouts, cut_neighbours(): jnp.roll(field, -1, 1)[1:-1]  8.11 us
    ppermute x3, starting transfers between devices, shifted(): return lax.ppermute(value, axis, pairs)  7.23 us
    ppermute x9, waiting for transfers between devices, with_halo(): lax.ppermute(lax.slice_in_dim(block, 0, width, axis=dim), axis, backward)  6.97 us
  transfers between devices with their start and end apart: 24, of which 21 were waited for; matrix products, arithmetic and copies ran while one was open for 1% of the time, Pallas kernels for 0%

profile of v1, /device:TPU:4, one launch (start us, length us, event | category | flops | bytes accessed | tf_op | source)
XLA Modules:
  0.0 139.0 jit_solution(15917465170785556836)
XLA Ops:
  2.2 1.7 %collective-permute-start = (f32[3,8,256]{2,1,0:T(8,128)S(1)}, f32[3,8,256]{2,1,0:T(8,128)S(1)}, u32[]{:S(2)}, u32[]{:S(2)}) collective-permute-start(f32[3,8,256]{2,1,0:T(8,128)S(1)} %get-tuple-element.365), channel_id=1, source_target_pairs={{0,1},{1,2},{2,3},{3,4},{4,5},{5,6},{6,7},{7,0},{8,9},{9,10},{10,1... | collective-permute-start | bytes 73736 | tf_op jit(solution)/shard_map/while/body/eval_jaxpr/ppermute | solution.py:19
  3.8 3.4 %collective-permute-start.4 = (f32[3,24,256]{2,1,0:T(8,128)S(1)}, f32[3,24,256]{2,1,0:T(8,128)S(1)}, u32[]{:S(2)}, u32[]{:S(2)}) collective-permute-start(f32[3,24,256]{2,1,0:T(8,128)S(1)} %bitcast.5629), channel_id=1, source_target_pairs={{0,8},{8,16},{16,24},{1,9},{9,17},{17,25},{2,10},{10,18},{18,26},{... | collective-permute-start | bytes 221192 | tf_op jit(solution)/shard_map/ppermute | solution.py:30
  7.2 1.6 %collective-permute-start.3 = (f32[8,256]{1,0:T(8,128)S(1)}, f32[8,256]{1,0:T(8,128)S(1)}, u32[]{:S(2)}, u32[]{:S(2)}) collective-permute-start(f32[8,256]{1,0:T(8,128)S(1)} %get-tuple-element.1258), channel_id=1, source_target_pairs={{1,0},{2,1},{3,2},{4,3},{5,4},{6,5},{7,6},{0,7},{9,8},{10,9},{11,1... | collective-permute-start | bytes 24584 | tf_op jit(solution)/shard_map/ppermute | solution.py:22
  12.1 3.6 %collective-permute-start.6 = (f32[3,8,256]{2,1,0:T(8,128)S(1)}, f32[3,8,256]{2,1,0:T(8,128)S(1)}, u32[]{:S(2)}, u32[]{:S(2)}) collective-permute-start(f32[3,8,256]{2,1,0:T(8,128)S(1)} %get-tuple-element.377), channel_id=1, source_target_pairs={{1,0},{2,1},{3,2},{4,3},{5,4},{6,5},{7,6},{0,7},{9,8},{10,9},{11,1... | collective-permute-start | bytes 73736 | tf_op jit(solution)/shard_map/ppermute | solution.py:22
  16.0 1.2 collective-permute-done.6
  17.2 3.5 %collective-permute-done.5 = f32[3,8,256]{2,1,0:T(8,128)S(1)} collective-permute-done((f32[3,8,256]{2,1,0:T(8,128)S(1)}, f32[3,8,256]{2,1,0:T(8,128)S(1)}, u32[]{:S(2)}, u32[]{:S(2)}) %collective-permute-start.5) | collective-permute-done | bytes 24608 | tf_op jit(solution)/shard_map/ppermute | solution.py:19
  29.3 0.9 collective-permute-done.8
  30.2 3.6 %collective-permute-done.7 = f32[3,8,256]{2,1,0:T(8,128)S(1)} collective-permute-done((f32[3,8,256]{2,1,0:T(8,128)S(1)}, f32[3,8,256]{2,1,0:T(8,128)S(1)}, u32[]{:S(2)}, u32[]{:S(2)}) %collective-permute-start.7) | collective-permute-done | bytes 24608 | tf_op jit(solution)/shard_map/ppermute | solution.py:19
  41.9 1.9 %collective-permute-start.9 = (f32[3,24,256]{2,1,0:T(8,128)S(1)}, f32[3,24,256]{2,1,0:T(8,128)S(1)}, u32[]{:S(2)}, u32[]{:S(2)}) collective-permute-start(f32[3,24,256]{2,1,0:T(8,128)S(1)} %fusion.57), channel_id=1, source_target_pairs={{0,8},{8,16},{16,24},{1,9},{9,17},{17,25},{2,10},{10,18},{18,26},{... | collective-permute-start | bytes 221192 | tf_op jit(solution)/shard_map/ppermute | solution.py:30
  43.9 5.1 %collective-permute-done.9 = f32[3,24,256]{2,1,0:T(8,128)S(1)} collective-permute-done((f32[3,24,256]{2,1,0:T(8,128)S(1)}, f32[3,24,256]{2,1,0:T(8,128)S(1)}, u32[]{:S(2)}, u32[]{:S(2)}) %collective-permute-start.9) | collective-permute-done | bytes 73760 | tf_op jit(solution)/shard_map/ppermute | solution.py:30
  49.7 0.9 collective-permute-done.11
  50.6 3.6 %collective-permute-done.10 = f32[3,8,256]{2,1,0:T(8,128)S(1)} collective-permute-done((f32[3,8,256]{2,1,0:T(8,128)S(1)}, f32[3,8,256]{2,1,0:T(8,128)S(1)}, u32[]{:S(2)}, u32[]{:S(2)}) %collective-permute-start.10) | collective-permute-done | bytes 24608 | tf_op jit(solution)/shard_map/ppermute | solution.py:19
  64.5 3.7 %collective-permute-done.12 = f32[3,8,256]{2,1,0:T(8,128)S(1)} collective-permute-done((f32[3,8,256]{2,1,0:T(8,128)S(1)}, f32[3,8,256]{2,1,0:T(8,128)S(1)}, u32[]{:S(2)}, u32[]{:S(2)}) %collective-permute-start.12) | collective-permute-done | bytes 24608 | tf_op jit(solution)/shard_map/ppermute | solution.py:19
  77.0 0.9 collective-permute-done.15
  78.0 3.6 %collective-permute-done.14 = f32[3,8,256]{2,1,0:T(8,128)S(1)} collective-permute-done((f32[3,8,256]{2,1,0:T(8,128)S(1)}, f32[3,8,256]{2,1,0:T(8,128)S(1)}, u32[]{:S(2)}, u32[]{:S(2)}) %collective-permute-start.14) | collective-permute-done | bytes 24608 | tf_op jit(solution)/shard_map/ppermute | solution.py:19
  81.7 6.7 %collective-permute-done.16 = f32[1,3,40,256]{3,2,1,0:T(8,128)S(1)} collective-permute-done((f32[1,3,40,256]{3,2,1,0:T(8,128)S(1)}, f32[1,3,40,256]{3,2,1,0:T(8,128)S(1)}, u32[]{:S(2)}, u32[]{:S(2)}) %collective-permute-start.16) | collective-permute-done | bytes 122912 | tf_op jit(solution)/shard_map/ppermute | solution.py:133
  88.5 6.2 %collective-permute-done.17 = f32[1,3,40,256]{3,2,1,0:T(8,128)S(1)} collective-permute-done((f32[1,3,40,256]{3,2,1,0:T(8,128)S(1)}, f32[1,3,40,256]{3,2,1,0:T(8,128)S(1)}, u32[]{:S(2)}, u32[]{:S(2)}) %collective-permute-start.17) | collective-permute-done | bytes 122912 | tf_op jit(solution)/shard_map/ppermute | solution.py:133
  94.8 5.7 %collective-permute-done.18 = f32[1,3,40,256]{3,2,1,0:T(8,128)S(1)} collective-permute-done((f32[1,3,40,256]{3,2,1,0:T(8,128)S(1)}, f32[1,3,40,256]{3,2,1,0:T(8,128)S(1)}, u32[]{:S(2)}, u32[]{:S(2)}) %collective-permute-start.18) | collective-permute-done | bytes 122912 | tf_op jit(solution)/shard_map/ppermute | solution.py:133
  106.8 1.9 %collective-permute-start.19 = (f32[3,24,256]{2,1,0:T(8,128)S(1)}, f32[3,24,256]{2,1,0:T(8,128)S(1)}, u32[]{:S(2)}, u32[]{:S(2)}) collective-permute-start(f32[3,24,256]{2,1,0:T(8,128)S(1)} %fusion.47), channel_id=1, source_target_pairs={{0,8},{8,16},{16,24},{1,9},{9,17},{17,25},{2,10},{10,18},{18,26},{... | collective-permute-start | bytes 221192 | tf_op jit(solution)/shard_map/ppermute | solution.py:30
  108.7 5.2 %collective-permute-done.19 = f32[3,24,256]{2,1,0:T(8,128)S(1)} collective-permute-done((f32[3,24,256]{2,1,0:T(8,128)S(1)}, f32[3,24,256]{2,1,0:T(8,128)S(1)}, u32[]{:S(2)}, u32[]{:S(2)}) %collective-permute-start.19) | collective-permute-done | bytes 73760 | tf_op jit(solution)/shard_map/ppermute | solution.py:30
  114.5 1.0 collective-permute-done.21
  115.5 3.6 %collective-permute-done.20 = f32[3,8,256]{2,1,0:T(8,128)S(1)} collective-permute-done((f32[3,8,256]{2,1,0:T(8,128)S(1)}, f32[3,8,256]{2,1,0:T(8,128)S(1)}, u32[]{:S(2)}, u32[]{:S(2)}) %collective-permute-start.20) | collective-permute-done | bytes 24608 | tf_op jit(solution)/shard_map/ppermute | solution.py:19
  127.8 1.0 collective-permute-done.23
  128.8 3.6 %collective-permute-done.22 = f32[3,6,256]{2,1,0:T(8,128)S(1)} collective-permute-done((f32[3,6,256]{2,1,0:T(8,128)S(1)}, f32[3,6,256]{2,1,0:T(8,128)S(1)}, u32[]{:S(2)}, u32[]{:S(2)}) %collective-permute-start.22) | collective-permute-done | bytes 18464 | tf_op jit(solution)/shard_map/ppermute | solution.py:19
  (830 shorter events, 61.8 us)
Async XLA Ops:
  1.4 8.3 %collective-permute-start.2 = (f32[8,256]{1,0:T(8,128)S(1)}, f32[8,256]{1,0:T(8,128)S(1)}, u32[]{:S(2)}, u32[]{:S(2)}) collective-permute-start(f32[8,256]{1,0:T(8,128)S(1)} %get-tuple-element.1259), channel_id=1, source_target_pairs={{0,1},{1,2},{2,3},{3,4},{4,5},{5,6},{6,7},{7,0},{8,9},{9,10},{10,1... | collective-permute-start | bytes 24584 | tf_op jit(solution)/shard_map/ppermute | solution.py:19
  2.2 8.3 %collective-permute-start = (f32[3,8,256]{2,1,0:T(8,128)S(1)}, f32[3,8,256]{2,1,0:T(8,128)S(1)}, u32[]{:S(2)}, u32[]{:S(2)}) collective-permute-start(f32[3,8,256]{2,1,0:T(8,128)S(1)} %get-tuple-element.365), channel_id=1, source_target_pairs={{0,1},{1,2},{2,3},{3,4},{4,5},{5,6},{6,7},{7,0},{8,9},{9,10},{10,1... | collective-permute-start | bytes 73736 | tf_op jit(solution)/shard_map/while/body/eval_jaxpr/ppermute | solution.py:19
  3.8 7.1 %collective-permute-start.4 = (f32[3,24,256]{2,1,0:T(8,128)S(1)}, f32[3,24,256]{2,1,0:T(8,128)S(1)}, u32[]{:S(2)}, u32[]{:S(2)}) collective-permute-start(f32[3,24,256]{2,1,0:T(8,128)S(1)} %bitcast.5629), channel_id=1, source_target_pairs={{0,8},{8,16},{16,24},{1,9},{9,17},{17,25},{2,10},{10,18},{18,26},{... | collective-permute-start | bytes 221192 | tf_op jit(solution)/shard_map/ppermute | solution.py:30
  7.2 3.2 %collective-permute-start.3 = (f32[8,256]{1,0:T(8,128)S(1)}, f32[8,256]{1,0:T(8,128)S(1)}, u32[]{:S(2)}, u32[]{:S(2)}) collective-permute-start(f32[8,256]{1,0:T(8,128)S(1)} %get-tuple-element.1258), channel_id=1, source_target_pairs={{1,0},{2,1},{3,2},{4,3},{5,4},{6,5},{7,6},{0,7},{9,8},{10,9},{11,1... | collective-permute-start | bytes 24584 | tf_op jit(solution)/shard_map/ppermute | solution.py:22
  8.9 2.3 %collective-permute-start.1 = (f32[3,8,256]{2,1,0:T(8,128)S(1)}, f32[3,8,256]{2,1,0:T(8,128)S(1)}, u32[]{:S(2)}, u32[]{:S(2)}) collective-permute-start(f32[3,8,256]{2,1,0:T(8,128)S(1)} %get-tuple-element.364), channel_id=1, source_target_pairs={{1,0},{2,1},{3,2},{4,3},{5,4},{6,5},{7,6},{0,7},{9,8},{10,9},{11,1... | collective-permute-start | bytes 73736 | tf_op jit(solution)/shard_map/while/body/eval_jaxpr/ppermute | solution.py:22
  12.1 5.1 %collective-permute-start.6 = (f32[3,8,256]{2,1,0:T(8,128)S(1)}, f32[3,8,256]{2,1,0:T(8,128)S(1)}, u32[]{:S(2)}, u32[]{:S(2)}) collective-permute-start(f32[3,8,256]{2,1,0:T(8,128)S(1)} %get-tuple-element.377), channel_id=1, source_target_pairs={{1,0},{2,1},{3,2},{4,3},{5,4},{6,5},{7,6},{0,7},{9,8},{10,9},{11,1... | collective-permute-start | bytes 73736 | tf_op jit(solution)/shard_map/ppermute | solution.py:22
  15.7 5.0 %collective-permute-start.5 = (f32[3,8,256]{2,1,0:T(8,128)S(1)}, f32[3,8,256]{2,1,0:T(8,128)S(1)}, u32[]{:S(2)}, u32[]{:S(2)}) collective-permute-start(f32[3,8,256]{2,1,0:T(8,128)S(1)} %get-tuple-element.376), channel_id=1, source_target_pairs={{0,1},{1,2},{2,3},{3,4},{4,5},{5,6},{6,7},{7,0},{8,9},{9,10},{10,1... | collective-permute-start | bytes 73736 | tf_op jit(solution)/shard_map/ppermute | solution.py:19
  28.7 1.6 %collective-permute-start.8 = (f32[3,8,256]{2,1,0:T(8,128)S(1)}, f32[3,8,256]{2,1,0:T(8,128)S(1)}, u32[]{:S(2)}, u32[]{:S(2)}) collective-permute-start(f32[3,8,256]{2,1,0:T(8,128)S(1)} %get-tuple-element.375), channel_id=1, source_target_pairs={{1,0},{2,1},{3,2},{4,3},{5,4},{6,5},{7,6},{0,7},{9,8},{10,9},{11,1... | collective-permute-start | bytes 73736 | tf_op jit(solution)/shard_map/ppermute | solution.py:22
  28.7 5.1 %collective-permute-start.7 = (f32[3,8,256]{2,1,0:T(8,128)S(1)}, f32[3,8,256]{2,1,0:T(8,128)S(1)}, u32[]{:S(2)}, u32[]{:S(2)}) collective-permute-start(f32[3,8,256]{2,1,0:T(8,128)S(1)} %get-tuple-element.374), channel_id=1, source_target_pairs={{0,1},{1,2},{2,3},{3,4},{4,5},{5,6},{6,7},{7,0},{8,9},{9,10},{10,1... | collective-permute-start | bytes 73736 | tf_op jit(solution)/shard_map/ppermute | solution.py:19
  41.9 7.1 %collective-permute-start.9 = (f32[3,24,256]{2,1,0:T(8,128)S(1)}, f32[3,24,256]{2,1,0:T(8,128)S(1)}, u32[]{:S(2)}, u32[]{:S(2)}) collective-permute-start(f32[3,24,256]{2,1,0:T(8,128)S(1)} %fusion.57), channel_id=1, source_target_pairs={{0,8},{8,16},{16,24},{1,9},{9,17},{17,25},{2,10},{10,18},{18,26},{... | collective-permute-start | bytes 221192 | tf_op jit(solution)/shard_map/ppermute | solution.py:30
  49.1 1.6 %collective-permute-start.11 = (f32[3,8,256]{2,1,0:T(8,128)S(1)}, f32[3,8,256]{2,1,0:T(8,128)S(1)}, u32[]{:S(2)}, u32[]{:S(2)}) collective-permute-start(f32[3,8,256]{2,1,0:T(8,128)S(1)} %get-tuple-element.373), channel_id=1, source_target_pairs={{1,0},{2,1},{3,2},{4,3},{5,4},{6,5},{7,6},{0,7},{9,8},{10,9},{11,1... | collective-permute-start | bytes 73736 | tf_op jit(solution)/shard_map/ppermute | solution.py:22
  49.1 5.1 %collective-permute-start.10 = (f32[3,8,256]{2,1,0:T(8,128)S(1)}, f32[3,8,256]{2,1,0:T(8,128)S(1)}, u32[]{:S(2)}, u32[]{:S(2)}) collective-permute-start(f32[3,8,256]{2,1,0:T(8,128)S(1)} %get-tuple-element.372), channel_id=1, source_target_pairs={{0,1},{1,2},{2,3},{3,4},{4,5},{5,6},{6,7},{7,0},{8,9},{9,10},{10,1... | collective-permute-start | bytes 73736 | tf_op jit(solution)/shard_map/ppermute | solution.py:19
  62.9 1.6 %collective-permute-start.13 = (f32[3,8,256]{2,1,0:T(8,128)S(1)}, f32[3,8,256]{2,1,0:T(8,128)S(1)}, u32[]{:S(2)}, u32[]{:S(2)}) collective-permute-start(f32[3,8,256]{2,1,0:T(8,128)S(1)} %get-tuple-element.371), channel_id=1, source_target_pairs={{1,0},{2,1},{3,2},{4,3},{5,4},{6,5},{7,6},{0,7},{9,8},{10,9},{11,1... | collective-permute-start | bytes 73736 | tf_op jit(solution)/shard_map/ppermute | solution.py:22
  63.0 5.3 %collective-permute-start.12 = (f32[3,8,256]{2,1,0:T(8,128)S(1)}, f32[3,8,256]{2,1,0:T(8,128)S(1)}, u32[]{:S(2)}, u32[]{:S(2)}) collective-permute-start(f32[3,8,256]{2,1,0:T(8,128)S(1)} %get-tuple-element.370), channel_id=1, source_target_pairs={{0,1},{1,2},{2,3},{3,4},{4,5},{5,6},{6,7},{7,0},{8,9},{9,10},{10,1... | collective-permute-start | bytes 73736 | tf_op jit(solution)/shard_map/ppermute | solution.py:19
  76.4 1.6 %collective-permute-start.15 = (f32[3,8,256]{2,1,0:T(8,128)S(1)}, f32[3,8,256]{2,1,0:T(8,128)S(1)}, u32[]{:S(2)}, u32[]{:S(2)}) collective-permute-start(f32[3,8,256]{2,1,0:T(8,128)S(1)} %get-tuple-element.369), channel_id=1, source_target_pairs={{1,0},{2,1},{3,2},{4,3},{5,4},{6,5},{7,6},{0,7},{9,8},{10,9},{11,1... | collective-permute-start | bytes 73736 | tf_op jit(solution)/shard_map/ppermute | solution.py:22
  76.4 5.1 %collective-permute-start.14 = (f32[3,8,256]{2,1,0:T(8,128)S(1)}, f32[3,8,256]{2,1,0:T(8,128)S(1)}, u32[]{:S(2)}, u32[]{:S(2)}) collective-permute-start(f32[3,8,256]{2,1,0:T(8,128)S(1)} %get-tuple-element.368), channel_id=1, source_target_pairs={{0,1},{1,2},{2,3},{3,4},{4,5},{5,6},{6,7},{7,0},{8,9},{9,10},{10,1... | collective-permute-start | bytes 73736 | tf_op jit(solution)/shard_map/ppermute | solution.py:19
  81.6 6.9 %collective-permute-start.16 = (f32[1,3,40,256]{3,2,1,0:T(8,128)S(1)}, f32[1,3,40,256]{3,2,1,0:T(8,128)S(1)}, u32[]{:S(2)}, u32[]{:S(2)}) collective-permute-start(f32[1,3,40,256]{3,2,1,0:T(8,128)S(1)} %maximum_bitcast_fusion), channel_id=1, source_target_pairs={{0,8},{8,16},{16,24},{24,0},{1,9},{9,17},{17,25},{25,1},{2,10},{10... | collective-permute-start | bytes 368648 | tf_op jit(solution)/shard_map/ppermute | solution.py:133
  88.5 6.2 %collective-permute-start.17 = (f32[1,3,40,256]{3,2,1,0:T(8,128)S(1)}, f32[1,3,40,256]{3,2,1,0:T(8,128)S(1)}, u32[]{:S(2)}, u32[]{:S(2)}) collective-permute-start(f32[1,3,40,256]{3,2,1,0:T(8,128)S(1)} %collective-permute-done.16), channel_id=1, source_target_pairs={{0,8},{8,16},{16,24},{24,0},{1,9},{9,17},{17,25},{25,1},{2,10},{10... | collective-permute-start | bytes 368648 | tf_op jit(solution)/shard_map/ppermute | solution.py:133
  94.7 5.8 %collective-permute-start.18 = (f32[1,3,40,256]{3,2,1,0:T(8,128)S(1)}, f32[1,3,40,256]{3,2,1,0:T(8,128)S(1)}, u32[]{:S(2)}, u32[]{:S(2)}) collective-permute-start(f32[1,3,40,256]{3,2,1,0:T(8,128)S(1)} %collective-permute-done.17), channel_id=1, source_target_pairs={{0,8},{8,16},{16,24},{24,0},{1,9},{9,17},{17,25},{25,1},{2,10},{10... | collective-permute-start | bytes 368648 | tf_op jit(solution)/shard_map/ppermute | solution.py:133
  106.8 7.1 %collective-permute-start.19 = (f32[3,24,256]{2,1,0:T(8,128)S(1)}, f32[3,24,256]{2,1,0:T(8,128)S(1)}, u32[]{:S(2)}, u32[]{:S(2)}) collective-permute-start(f32[3,24,256]{2,1,0:T(8,128)S(1)} %fusion.47), channel_id=1, source_target_pairs={{0,8},{8,16},{16,24},{1,9},{9,17},{17,25},{2,10},{10,18},{18,26},{... | collective-permute-start | bytes 221192 | tf_op jit(solution)/shard_map/ppermute | solution.py:30
  114.0 1.6 %collective-permute-start.21 = (f32[3,8,256]{2,1,0:T(8,128)S(1)}, f32[3,8,256]{2,1,0:T(8,128)S(1)}, u32[]{:S(2)}, u32[]{:S(2)}) collective-permute-start(f32[3,8,256]{2,1,0:T(8,128)S(1)} %get-tuple-element.363), channel_id=1, source_target_pairs={{1,0},{2,1},{3,2},{4,3},{5,4},{6,5},{7,6},{0,7},{9,8},{10,9},{11,1... | collective-permute-start | bytes 73736 | tf_op jit(solution)/shard_map/ppermute | solution.py:22
  114.0 5.1 %collective-permute-start.20 = (f32[3,8,256]{2,1,0:T(8,128)S(1)}, f32[3,8,256]{2,1,0:T(8,128)S(1)}, u32[]{:S(2)}, u32[]{:S(2)}) collective-permute-start(f32[3,8,256]{2,1,0:T(8,128)S(1)} %get-tuple-element.362), channel_id=1, source_target_pairs={{0,1},{1,2},{2,3},{3,4},{4,5},{5,6},{6,7},{7,0},{8,9},{9,10},{10,1... | collective-permute-start | bytes 73736 | tf_op jit(solution)/shard_map/ppermute | solution.py:19
  127.2 1.6 %collective-permute-start.23 = (f32[3,6,256]{2,1,0:T(8,128)S(1)}, f32[3,6,256]{2,1,0:T(8,128)S(1)}, u32[]{:S(2)}, u32[]{:S(2)}) collective-permute-start(f32[3,6,256]{2,1,0:T(8,128)S(1)} %get-tuple-element.361), channel_id=1, source_target_pairs={{1,0},{2,1},{3,2},{4,3},{5,4},{6,5},{7,6},{0,7},{9,8},{10,9},{11,1... | collective-permute-start | bytes 55304 | tf_op jit(solution)/shard_map/ppermute | solution.py:22
  127.3 5.1 %collective-permute-start.22 = (f32[3,6,256]{2,1,0:T(8,128)S(1)}, f32[3,6,256]{2,1,0:T(8,128)S(1)}, u32[]{:S(2)}, u32[]{:S(2)}) collective-permute-start(f32[3,6,256]{2,1,0:T(8,128)S(1)} %get-tuple-element.360), channel_id=1, source_target_pairs={{0,1},{1,2},{2,3},{3,4},{4,5},{5,6},{6,7},{7,0},{8,9},{9,10},{10,1... | collective-permute-start | bytes 55304 | tf_op jit(solution)/shard_map/ppermute | solution.py:19
  (4 other events, 12.5 us)
